TPU v7x, 256 devices: a 4x2x16 block of a 4x16x16 slice. The times are simulated.
256 devices in a mesh: pb: 2 (over y), col: 32 (over z, core), row: 4 (over x).
Axes of the slice: x: 4, y: 2, z: 16, core: 2. Of those that a mesh axis runs over, the one named last changes fastest.
The devices are a block of a 4x16x16 slice.
Arguments:
- pair_density: bfloat16 [6144, 6144], P(('pb', 'col'), 'row'), parts along dimension 0, may hold values from -0.19921875 to 0.19921875
- band_pairs: int32 [2, 3072], replicated, may hold values from 0 to 255, as said below
- valence: float32 [256], replicated, may hold values from -12 to -2
- conduction: float32 [12], replicated, may hold values from 1 to 8
- wave_vectors: int32 [3, 12288], P(None, 'pb'), parts along dimension 1, may hold values from -6 to 6
- momentum: float32 [6], P('pb'), parts along dimension 0, may hold values from 0.3 to 0.7
- guess_scale: float32 [12288], P('pb'), parts along dimension 0, may hold values from 0.4 to 0.75
Outputs:
- epsilon: float32 [12288, 6144], P(('pb', 'row'), 'col'), parts along dimension 0
- inverse: float32 [12288, 6144], P(('pb', 'row'), 'col'), parts along dimension 0
There are 2 independent parts, one for each index of `pb`. A program takes and returns all parts, laid end to end along the dimension named above; an argument that names none is the same for every part. Nothing has to cross between parts.
Inputs may be any that keep to these rules, and one draw needn't show every extreme that they name: `band_pairs`: column p names a valence band below 256 in row 0 and a conduction band below 12 in row 1; every such pair of bands appears in exactly one column.
All inputs are finite; a program needn't handle non-finite values.
Results may differ from a plain program's by a relative error of at most 0.0036.
The roundings to bfloat16 on the way count: a program that leaves them out, or rounds other values in their place, can miss the bound.
Values may be sent and summed in bfloat16 or wider, within the bound.
A program may use at most 64 MiB of HBM per device.

v0:
```python
import math
import jax
import jax.numpy as jnp
from jax import lax
from jax.sharding import PartitionSpec as P


def lookup(indices, table):
    levels = jnp.arange(table.shape[0], dtype=jnp.int32)
    picked = indices[:, None] == levels[None, :]
    return jnp.sum(jnp.where(picked, table[None, :], 0.0), axis=1)


def on_device(pair_density, band_pairs, valence, conduction, wave_vectors, momentum, guess_scale):
    column_index = lax.axis_index("col")
    row_index = lax.axis_index("row")
    row_height = pair_density.shape[1]
    whole_width = row_height * lax.axis_size("row")
    strip_width = whole_width // lax.axis_size("col")
    valence_of = lookup(band_pairs[0], valence)
    conduction_of = lookup(band_pairs[1], conduction)
    weight = 4.0 / (valence_of - conduction_of)
    shifted = wave_vectors.astype(jnp.float32) + momentum[:, None]
    sqrt_all = jnp.sqrt(4.0 * math.pi / jnp.sum(shifted * shifted, axis=0))
    row_first = row_index * row_height
    column_first = column_index * strip_width
    sqrt_rows = lax.dynamic_slice_in_dim(sqrt_all, row_first, row_height, 0)
    sqrt_cols = lax.dynamic_slice_in_dim(sqrt_all, column_first, strip_width, 0)
    scale_rows = lax.dynamic_slice_in_dim(guess_scale, row_first, row_height, 0)
    scale_cols = lax.dynamic_slice_in_dim(guess_scale, column_first, strip_width, 0)
    panel_pairs = lax.all_gather(pair_density, "col", axis=0, tiled=True)
    owner = column_first // row_height
    offset = column_first % row_height
    own_slice = lax.dynamic_slice_in_dim(panel_pairs, offset, strip_width, 1)
    candidates = lax.all_gather(own_slice, "row", axis=1, tiled=True)
    strip_pairs = lax.dynamic_slice_in_dim(candidates, owner * strip_width, strip_width, 1)
    weighted = (weight[:, None] * panel_pairs.astype(jnp.float32)).astype(jnp.bfloat16)
    weighted_strip = (weight[:, None] * strip_pairs.astype(jnp.float32)).astype(jnp.bfloat16)
    chi_block = lax.dot_general(
        weighted, strip_pairs, (((0,), (0,)), ((), ())), preferred_element_type=jnp.float32
    )
    chi_rows = jnp.sum(weighted.astype(jnp.float32) * panel_pairs.astype(jnp.float32), axis=0)
    chi_cols = jnp.sum(weighted_strip.astype(jnp.float32) * strip_pairs.astype(jnp.float32), axis=0)
    global_rows = row_first + jnp.arange(row_height, dtype=jnp.int32)
    global_cols = column_first + jnp.arange(strip_width, dtype=jnp.int32)
    identity = (global_rows[:, None] == global_cols[None, :]).astype(jnp.float32)
    epsilon = identity - sqrt_rows[:, None] * chi_block * sqrt_cols[None, :]
    diagonal_rows = 1.0 - sqrt_rows * chi_rows * sqrt_rows
    guess_rows = scale_rows / diagonal_rows
    guess_cols = scale_cols / (1.0 - sqrt_cols * chi_cols * sqrt_cols)
    mixed = epsilon * guess_cols[None, :]
    mixed_b = mixed.astype(jnp.bfloat16)
    mixed_diagonal = diagonal_rows * guess_rows
    rounded_diagonal = mixed_diagonal.astype(jnp.bfloat16).astype(jnp.float32)
    delta = guess_rows + (rounded_diagonal - mixed_diagonal)
    inner = sqrt_rows * guess_rows

    def times_mixed(block):
        wide = block.astype(jnp.float32)
        scaled = (inner[:, None] * wide).astype(jnp.bfloat16)
        partial = jnp.dot(panel_pairs, scaled, preferred_element_type=jnp.float32)
        total = lax.psum(partial.astype(jnp.bfloat16), "row")
        spread = lax.dot_general(
            weighted, total, (((0,), (0,)), ((), ())), preferred_element_type=jnp.float32
        )
        return delta[:, None] * wide - sqrt_rows[:, None] * spread

    square = times_mixed(mixed_b)
    cube = times_mixed(square.astype(jnp.bfloat16))
    inverse = guess_rows[:, None] * (4.0 * identity - 6.0 * mixed + 4.0 * square - cube)
    return (epsilon, inverse)


def solution(mesh):
    placed = (P(("pb", "col"), "row"), P(), P(), P(), P(None, "pb"), P("pb"), P("pb"))
    return jax.shard_map(
        on_device,
        mesh=mesh,
        in_specs=placed,
        out_specs=(P(("pb", "row"), "col"), P(("pb", "row"), "col")),
        check_vma=False,
    )
```

profile of v0, /device:TPU:33, one launch (start us, length us, event | category | flops | bytes accessed | tf_op | source)
XLA Modules:
  0.0 317.8 jit_solution(16853335193049921923)
XLA Ops:
  7.2 0.1 all-gather.3.cloned.1.call-start
  7.2 0.7 all-gather.3.cloned.1.call-update
  8.0 0.1 all-gather.5.cloned.1.call-start
  8.1 94.8 %all-gather.3.cloned.1.call-done = bf16[3072,1536]{1,0:T(8,128)(2,1)} async-done(((bf16[96,1536]{1,0:T(8,128)(2,1)}), bf16[3072,1536]{1,0:T(8,128)(2,1)}) %all-gather.3.cloned.1.call-update) | async-done | bytes 9437200 | tf_op jit(solution)/shard_map/all_gather | solution.py:31
  102.8 2.4 constant_dynamic-slice_fusion
  105.3 1.5 copy.11
  106.7 0.0 copy-start.1
  106.7 0.0 copy-start.4
  106.7 0.0 copy-start
  106.7 0.0 copy-start.3
  106.8 0.0 copy-start.2
  106.8 0.1 all-gather.5.cloned.1.call-update
  106.8 0.1 all-reduce.3.cloned.1.call-start
  106.9 0.5 copy-done.1
  107.5 0.0 copy-done.4
  107.5 0.1 select_reduce_fusion.1
  107.6 0.0 copy-done
  107.7 0.0 copy-done.3
  107.7 0.1 multiply_reduce_fusion
  107.8 0.0 copy-done.2
  107.8 1.9 select_reduce_fusion
  109.7 6.2 %fusion.1 = f32[1536]{0:T(1024)S(1)} fusion(bf16[3072,1536]{1,0:T(8,128)(2,1)} %all-gather.3.cloned.1.call-done, f32[3072]{0:T(1024)S(1)} %subtract_divide_fusion), kind=kLoop, calls=%fused_computation.3 | loop fusion | flops 28310016 | bytes 9455616 | tf_op jit(solution)/shard_map/reduce_sum | solution.py:42
  116.0 0.8 subtract_add_fusion
  116.8 44.2 %all-gather.5.cloned.1.call-done = bf16[3072,768]{0,1:T(8,128)(2,1)} async-done(((bf16[3072,192]{0,1:T(8,128)(2,1)}), bf16[3072,768]{0,1:T(8,128)(2,1)}) %all-gather.5.cloned.1.call-update) | async-done | bytes 4718608 | tf_op jit(solution)/shard_map/all_gather | solution.py:35
  161.0 0.0 slice-start
  161.0 1.8 fusion.11
  162.8 0.8 fusion.24
  163.6 0.0 slice-start.1
  163.6 0.0 slice-start.2
  163.6 6.5 %fusion.5 = f32[1536,192]{0,1:T(8,128)S(1)} fusion(bf16[3072,768]{0,1:T(8,128)(2,1)} %all-gather.5.cloned.1.call-done, s32[]{:T(128)S(6)} %select_n.39, f32[192]{0:T(256)S(1)} %get-tuple-element.6, f32[1536]{0:T(1024)S(1)} %get-tuple-element.4, s32[1536]{0:T(1024)S(1)} %iota_add_fusion, s32[192]{0:T(256)S(1)} %iota_add_fusion.1, ...), kind=kOutput, calls=%fused_computation.16 | convolution fusion | flops 1827569664 | bytes 11822596 | tf_op jit(solution)/shard_map/dot_general | solution.py:39
  170.1 0.0 copy-start.5
  170.1 0.0 slice-done
  170.1 0.0 slice-done.1
  170.1 0.0 slice-done.2
  170.1 4.3 %fusion.2 = bf16[3072,192]{0,1:T(8,128)(2,1)} fusion(bf16[3072,1536]{1,0:T(8,128)(2,1)S(1)} %bitcast.11, f32[1536]{0:T(1024)S(1)} %mul.163, f32[1536,192]{0,1:T(8,128)S(1)} %fusion.5, f32[192]{0:T(256)S(1)} %get-tuple-element.5), kind=kOutput, calls=%fused_computation.6 | convolution fusion | flops 1814003712 | bytes 11803392 | tf_op jit(solution)/shard_map/dot_general | solution.py:61
  174.4 0.0 slice-start.3
  174.4 0.1 all-reduce.3.cloned.1.call-update
  174.4 0.2 all-reduce.5.cloned.1.call-start
  174.7 58.0 %all-reduce.3.cloned.1.call-done = bf16[3072,192]{0,1:T(8,128)(2,1)} async-done(((bf16[3072,192]{0,1:T(8,128)(2,1)}), bf16[3072,192]{0,1:T(8,128)(2,1)}) %all-reduce.3.cloned.1.call-update) | async-done | bytes 1179664 | tf_op jit(solution)/shard_map/psum | solution.py:62
  232.7 0.0 slice-start.4
  232.7 0.0 slice-start.5
  232.7 6.5 %fusion.6 = f32[1536,192]{0,1:T(8,128)S(1)} fusion(bf16[3072,192]{0,1:T(8,128)(2,1)} %all-reduce.3.cloned.1.call-done, f32[1536]{0:T(1024)S(1)} %get-tuple-element.2, f32[1536]{0:T(1024)S(1)} %get-tuple-element.4, f32[1536,192]{0,1:T(8,128)S(1)} %fusion.5, f32[192]{0:T(256)S(1)} %get-tuple-element.5, bf16[3072,1536]{1,0:T(8,128)(2,1)} %all-gather.3.cloned.1.call-done, ...), kind=kOutput, calls=%fused_computation.17 | convolution fusion | flops 1827864576 | bytes 13001472 | tf_op jit(solution)/shard_map/dot_general | solution.py:63
  239.2 0.0 slice-done.3
  239.3 0.0 slice-done.4
  239.3 0.0 slice-done.5
  239.3 4.2 %fusion.3 = bf16[3072,192]{0,1:T(8,128)(2,1)} fusion(bf16[3072,1536]{1,0:T(8,128)(2,1)S(1)} %bitcast.13, f32[1536]{0:T(1024)S(1)} %mul.163, f32[1536,192]{0,1:T(8,128)S(1)} %fusion.6), kind=kOutput, calls=%fused_computation.7 | convolution fusion | flops 1813708800 | bytes 11802624 | tf_op jit(solution)/shard_map/dot_general | solution.py:61
  243.5 0.1 all-reduce.5.cloned.1.call-update
  243.6 59.8 %all-reduce.5.cloned.1.call-done = bf16[3072,192]{0,1:T(8,128)(2,1)} async-done(((bf16[3072,192]{0,1:T(8,128)(2,1)}), bf16[3072,192]{0,1:T(8,128)(2,1)}) %all-reduce.5.cloned.1.call-update) | async-done | bytes 1179664 | tf_op jit(solution)/shard_map/psum | solution.py:62
  303.4 0.0 copy-done.5
  303.4 7.8 %fusion.9 = f32[1536,192]{0,1:T(8,128)} fusion(bf16[3072,192]{0,1:T(8,128)(2,1)} %all-reduce.5.cloned.1.call-done, f32[1536,192]{0,1:T(8,128)S(1)} %fusion.6, f32[1536,192]{0,1:T(8,128)S(1)} %fusion.5, f32[1536]{0:T(1024)S(1)} %get-tuple-element.2, f32[192]{0:T(256)S(1)} %get-tuple-element.5, f32[1536]{0:T(1024)S(1)} %get-tuple-element.3, ...), kind=kOutput, calls=%fused_computation.20 | convolution fusion | flops 1830223872 | bytes 14194176 | tf_op jit(solution)/shard_map/dot_general | solution.py:63
  (8 shorter events, 0.1 us)
Async XLA Ops:
  7.2 95.7 %all-gather.3.cloned.1.call-start = ((), (), s32[]{:S(2)}) async-start(), calls=%async_computation | async-start | bytes 9732096 | tf_op jit(solution)/shard_map/all_gather | solution.py:31
  8.0 153.0 %all-gather.5.cloned.1.call-start = ((), (), s32[]{:S(2)}) async-start(), calls=%async_computation.1 | async-start | bytes 5898240 | tf_op jit(solution)/shard_map/all_gather | solution.py:35
  106.7 0.7 copy-start.1
  106.7 0.8 copy-start.4
  106.7 0.9 copy-start
  106.7 0.9 copy-start.3
  106.8 1.1 copy-start.2
  106.8 125.9 %all-reduce.3.cloned.1.call-start = ((), (), s32[]{:S(2)}) async-start(), calls=%async_computation.2 | async-start | bytes 2359296 | tf_op jit(solution)/shard_map/psum | solution.py:62
  161.0 9.1 %slice-start = ((s8[9437184]{0:T(1024)(128)(4,1)}), s8[4194304]{0:T(1024)(128)(4,1)S(1)}, s32[]{:S(2)}) async-start(s8[9437184]{0:T(1024)(128)(4,1)} %bitcast.10), calls=%async_computation.4 | async-start | bytes 8388608
  163.6 6.5 %slice-start.1 = ((s8[9437184]{0:T(1024)(128)(4,1)}), s8[4194304]{0:T(1024)(128)(4,1)S(1)}, s32[]{:S(2)}) async-start(s8[9437184]{0:T(1024)(128)(4,1)} %bitcast.10), calls=%async_computation.5 | async-start | bytes 8388608
  163.6 6.5 %slice-start.2 = ((s8[9437184]{0:T(1024)(128)(4,1)}), s8[1048576]{0:T(1024)(128)(4,1)S(1)}, s32[]{:S(2)}) async-start(s8[9437184]{0:T(1024)(128)(4,1)} %bitcast.10), calls=%async_computation.6 | async-start | bytes 2097152
  170.1 133.4 %copy-start.5 = (f32[1536,192]{0,1:T(8,128)}, f32[1536,192]{0,1:T(8,128)S(1)}, u32[]{:S(2)}) copy-start(f32[1536,192]{0,1:T(8,128)S(1)} %fusion.5) | copy-start | bytes 3538948
  174.4 64.9 %slice-start.3 = ((s8[9437184]{0:T(1024)(128)(4,1)}), s8[1048576]{0:T(1024)(128)(4,1)S(1)}, s32[]{:S(2)}) async-start(s8[9437184]{0:T(1024)(128)(4,1)} %bitcast.12), calls=%async_computation.7 | async-start | bytes 2097152
  174.4 129.0 %all-reduce.5.cloned.1.call-start = ((), (), s32[]{:S(2)}) async-start(), calls=%async_computation.3 | async-start | bytes 2359296 | tf_op jit(solution)/shard_map/psum | solution.py:62
  232.7 6.5 %slice-start.4 = ((s8[9437184]{0:T(1024)(128)(4,1)}), s8[4194304]{0:T(1024)(128)(4,1)S(1)}, s32[]{:S(2)}) async-start(s8[9437184]{0:T(1024)(128)(4,1)} %bitcast.12), calls=%async_computation.8 | async-start | bytes 8388608
  232.7 6.5 %slice-start.5 = ((s8[9437184]{0:T(1024)(128)(4,1)}), s8[4194304]{0:T(1024)(128)(4,1)S(1)}, s32[]{:S(2)}) async-start(s8[9437184]{0:T(1024)(128)(4,1)} %bitcast.12), calls=%async_computation.9 | async-start | bytes 8388608
Sparse Core Ops, SparseCore 0:
  9.9 92.9 all-gather.2
  106.9 53.9 all-gather.4
  174.6 58.1 all-reduce.2
  243.7 59.6 all-reduce.4
where the time goes:
time: 318 us
  waiting for transfers between devices  258 us (81%)
  matrix products  29.3 us (9%)
  between operations  14 us (4%)
  other arithmetic  11.8 us (4%)
  local copies, waits for them, and re-layouts  4.54 us (1%)
    psum x2, waiting for transfers between devices, times_mixed(): total = lax.psum(partial.astype(jnp.bfloat16), 'row')  118 us
    all_gather x1, waiting for transfers between devices, on_device(): panel_pairs = lax.all_gather(pair_density, 'col', axis=0, tiled=True)  94.8 us
    all_gather x1, waiting for transfers between devices, on_device(): candidates = lax.all_gather(own_slice, 'row', axis=1, tiled=True)  44.2 us
    dot_general x2, matrix products, times_mixed(): lax.dot_general(weighted, total, (((0,), (0,)), ((), ())), preferred_elem...  14.3 us
    dot_general x2, matrix products, times_mixed(): partial = jnp.dot(panel_pairs, scaled, preferred_element_type=jnp.float32)  8.49 us
    dot_general x1, matrix products, on_device(): lax.dot_general(weighted, strip_pairs, (((0,), (0,)), ((), ())), preferre...  6.49 us
  transfers between devices with their start and end apart: 4, of which 4 were waited for; matrix products, arithmetic and copies ran while one was open for 3% of the time, Pallas kernels for 0%

commit v1 on v0

--- a/solution.py
+++ b/solution.py
@@ -3,6 +3,12 @@
 import jax.numpy as jnp
 from jax import lax
 from jax.sharding import PartitionSpec as P
+
+
+def add_all(x, mesh_axis):
+    blocks = lax.all_gather(x, mesh_axis, axis=0, tiled=False)
+    result = blocks.sum(axis=0)
+    return result
 
 
 def lookup(indices, table):
@@ -59,7 +65,7 @@
         wide = block.astype(jnp.float32)
         scaled = (inner[:, None] * wide).astype(jnp.bfloat16)
         partial = jnp.dot(panel_pairs, scaled, preferred_element_type=jnp.float32)
-        total = lax.psum(partial.astype(jnp.bfloat16), "row")
+        total = add_all(partial.astype(jnp.bfloat16), "row")
         spread = lax.dot_general(
             weighted, total, (((0,), (0,)), ((), ())), preferred_element_type=jnp.float32
         )

time: 318 us -> 352 us (1.11)
  local copies, waits for them, and re-layouts: 4.54 us -> 22 us
  other arithmetic: 11.8 us -> 28 us
    all_gather x0 -> x2, waiting for transfers between devices: none -> 118 us  [add_all(): blocks = lax.all_gather(x, mesh_axis, axis=0, tiled=False)]
    psum x2 -> x0, waiting for transfers between devices: 118 us -> none  [times_mixed(): total = lax.psum(partial.astype(jnp.bfloat16), 'row')]
    all_gather x0 -> x2, local copies, waits for them, and re-layouts: none -> 16.4 us  [add_all(): blocks = lax.all_gather(x, mesh_axis, axis=0, tiled=False)]
    reduce_sum x0 -> x2, other arithmetic: none -> 16.2 us  [add_all(): result = blocks.sum(axis=0)]
where the time goes in v1:
time: 352 us
  waiting for transfers between devices  258 us (73%)
  matrix products  29.2 us (8%)
  other arithmetic  28 us (8%)
  local copies, waits for them, and re-layouts  22 us (6%)
  between operations  14 us (4%)
    all_gather x2, waiting for transfers between devices, add_all(): blocks = lax.all_gather(x, mesh_axis, axis=0, tiled=False)  118 us
    all_gather x1, waiting for transfers between devices, on_device(): panel_pairs = lax.all_gather(pair_density, 'col', axis=0, tiled=True)  94.8 us
    all_gather x1, waiting for transfers between devices, on_device(): candidates = lax.all_gather(own_slice, 'row', axis=1, tiled=True)  44.2 us
    all_gather x2, local copies, waits for them, and re-layouts, add_all(): blocks = lax.all_gather(x, mesh_axis, axis=0, tiled=False)  16.4 us
    reduce_sum x2, other arithmetic, add_all(): result = blocks.sum(axis=0)  16.2 us
    dot_general x2, matrix products, times_mixed(): lax.dot_general(weighted, total, (((0,), (0,)), ((), ())), preferred_elem...  14.2 us
    dot_general x2, matrix products, times_mixed(): partial = jnp.dot(panel_pairs, scaled, preferred_element_type=jnp.float32)  8.5 us
  transfers between devices with their start and end apart: 4, of which 4 were waited for; matrix products, arithmetic and copies ran while one was open for 3% of the time, Pallas kernels for 0%

profile of v1, /device:TPU:33, one launch (start us, length us, event | category | flops | bytes accessed | tf_op | source)
XLA Modules:
  0.0 351.7 jit_solution(10672955025727707169)
XLA Ops:
  7.2 0.1 all-gather.7.cloned.1.call-start
  7.2 0.7 all-gather.7.cloned.1.call-update
  8.0 0.1 all-gather.9.cloned.1.call-start
  8.1 94.8 %all-gather.7.cloned.1.call-done = bf16[3072,1536]{1,0:T(8,128)(2,1)} async-done(((bf16[96,1536]{1,0:T(8,128)(2,1)}), bf16[3072,1536]{1,0:T(8,128)(2,1)}) %all-gather.7.cloned.1.call-update) | async-done | bytes 9437200 | tf_op jit(solution)/shard_map/all_gather | solution.py:37
  102.8 2.4 constant_dynamic-slice_fusion
  105.3 1.5 copy.11
  106.7 0.0 copy-start.1
  106.7 0.0 copy-start.4
  106.7 0.0 copy-start
  106.7 0.0 copy-start.3
  106.8 0.0 copy-start.2
  106.8 0.1 all-gather.9.cloned.1.call-update
  106.8 0.1 all-gather.11.cloned.1.call-start
  106.9 0.5 copy-done.1
  107.5 0.0 copy-done.4
  107.5 0.1 select_reduce_fusion.1
  107.6 0.0 copy-done
  107.7 0.0 copy-done.3
  107.7 0.1 multiply_reduce_fusion
  107.8 0.0 copy-done.2
  107.8 1.9 select_reduce_fusion
  109.7 6.2 %fusion.1 = f32[1536]{0:T(1024)S(1)} fusion(bf16[3072,1536]{1,0:T(8,128)(2,1)} %all-gather.7.cloned.1.call-done, f32[3072]{0:T(1024)S(1)} %subtract_divide_fusion), kind=kLoop, calls=%fused_computation.3 | loop fusion | flops 28310016 | bytes 9455616 | tf_op jit(solution)/shard_map/reduce_sum | solution.py:48
  116.0 0.8 subtract_add_fusion
  116.8 44.2 %all-gather.9.cloned.1.call-done = bf16[3072,768]{0,1:T(8,128)(2,1)} async-done(((bf16[3072,192]{0,1:T(8,128)(2,1)}), bf16[3072,768]{0,1:T(8,128)(2,1)}) %all-gather.9.cloned.1.call-update) | async-done | bytes 4718608 | tf_op jit(solution)/shard_map/all_gather | solution.py:41
  161.0 0.0 slice-start
  161.0 1.8 fusion.11
  162.8 0.8 fusion.24
  163.6 0.0 slice-start.1
  163.6 0.0 slice-start.2
  163.6 6.5 %fusion.5 = f32[1536,192]{0,1:T(8,128)S(1)} fusion(bf16[3072,768]{0,1:T(8,128)(2,1)} %all-gather.9.cloned.1.call-done, s32[]{:T(128)S(6)} %select_n.39, f32[192]{0:T(256)S(1)} %get-tuple-element.6, f32[1536]{0:T(1024)S(1)} %get-tuple-element.4, s32[1536]{0:T(1024)S(1)} %iota_add_fusion, s32[192]{0:T(256)S(1)} %iota_add_fusion.1, ...), kind=kOutput, calls=%fused_computation.16 | convolution fusion | flops 1827569664 | bytes 11822596 | tf_op jit(solution)/shard_map/dot_general | solution.py:45
  170.1 0.0 copy-start.5
  170.1 0.0 slice-done
  170.1 0.0 slice-done.1
  170.1 0.0 slice-done.2
  170.1 4.3 %fusion.2 = bf16[3072,192]{0,1:T(8,128)(2,1)} fusion(bf16[3072,1536]{1,0:T(8,128)(2,1)S(1)} %bitcast.15, f32[1536]{0:T(1024)S(1)} %mul.163, f32[1536,192]{0,1:T(8,128)S(1)} %fusion.5, f32[192]{0:T(256)S(1)} %get-tuple-element.5), kind=kOutput, calls=%fused_computation.6 | convolution fusion | flops 1814003712 | bytes 11803392 | tf_op jit(solution)/shard_map/dot_general | solution.py:67
  174.4 0.1 all-gather.11.cloned.1.call-update
  174.4 0.2 all-gather.13.cloned.1.call-start
  174.7 59.0 %all-gather.11.cloned.1.call-done = bf16[12288,192]{0,1:T(8,128)(2,1)} async-done(((bf16[3072,192]{0,1:T(8,128)(2,1)}), bf16[12288,192]{0,1:T(8,128)(2,1)}) %all-gather.11.cloned.1.call-update) | async-done | bytes 4718608 | tf_op jit(solution)/shard_map/all_gather | solution.py:9
  233.7 8.2 %reshape.29 = bf16[4,3072,192]{1,0,2:T(4,128)(2,1)} reshape(bf16[12288,192]{0,1:T(8,128)(2,1)} %all-gather.11.cloned.1.call-done) | data formatting | bytes 9437184 | tf_op jit(solution)/shard_map/all_gather | solution.py:9
  241.9 0.0 slice-start.3
  241.9 8.1 %reduce_sum.74 = bf16[3072,192]{0,1:T(8,128)(2,1)S(1)} reduce(bf16[4,3072,192]{1,0,2:T(4,128)(2,1)} %reshape.29, bf16[]{:T(256)} %constant.49.clone.1), dimensions={0}, to_apply=%region_5.6 | reduce | flops 1769472 | bytes 5898242 | tf_op jit(solution)/shard_map/reduce_sum | solution.py:10
  250.0 0.0 slice-start.4
  250.0 0.0 slice-start.5
  250.1 6.1 %fusion.6 = f32[1536,192]{0,1:T(8,128)S(1)} fusion(bf16[3072,192]{0,1:T(8,128)(2,1)S(1)} %reduce_sum.74, f32[1536]{0:T(1024)S(1)} %get-tuple-element.2, f32[1536]{0:T(1024)S(1)} %get-tuple-element.4, f32[1536,192]{0,1:T(8,128)S(1)} %fusion.5, f32[192]{0:T(256)S(1)} %get-tuple-element.5, bf16[3072,1536]{1,0:T(8,128)(2,1)} %all-gather.7.cloned.1.call-done, ...), kind=kOutput, calls=%fused_computation.17 | convolution fusion | flops 1827864576 | bytes 13001472 | tf_op jit(solution)/shard_map/dot_general | solution.py:69
  256.2 0.0 copy-start.6
  256.2 1.0 copy-done.6
  257.2 0.0 slice-done.3
  257.2 0.0 slice-done.4
  257.2 0.0 slice-done.5
  257.2 4.2 %fusion.3 = bf16[3072,192]{0,1:T(8,128)(2,1)} fusion(bf16[3072,1536]{1,0:T(8,128)(2,1)S(1)} %bitcast.17, f32[1536]{0:T(1024)S(1)} %mul.163, f32[1536,192]{0,1:T(8,128)S(1)} %fusion.6), kind=kOutput, calls=%fused_computation.7 | convolution fusion | flops 1813708800 | bytes 11802624 | tf_op jit(solution)/shard_map/dot_general | solution.py:67
  261.5 0.1 all-gather.13.cloned.1.call-update
  261.5 59.2 %all-gather.13.cloned.1.call-done = bf16[12288,192]{0,1:T(8,128)(2,1)} async-done(((bf16[3072,192]{0,1:T(8,128)(2,1)}), bf16[12288,192]{0,1:T(8,128)(2,1)}) %all-gather.13.cloned.1.call-update) | async-done | bytes 4718608 | tf_op jit(solution)/shard_map/all_gather | solution.py:9
  320.8 8.2 %reshape.30 = bf16[4,3072,192]{1,0,2:T(4,128)(2,1)} reshape(bf16[12288,192]{0,1:T(8,128)(2,1)} %all-gather.13.cloned.1.call-done) | data formatting | bytes 9437184 | tf_op jit(solution)/shard_map/all_gather | solution.py:9
  329.0 8.1 %reduce_sum.75 = bf16[3072,192]{0,1:T(8,128)(2,1)S(1)} reduce(bf16[4,3072,192]{1,0,2:T(4,128)(2,1)} %reshape.30, bf16[]{:T(256)} %constant.49.clone.1), dimensions={0}, to_apply=%region_6.7 | reduce | flops 1769472 | bytes 5898242 | tf_op jit(solution)/shard_map/reduce_sum | solution.py:10
  337.0 0.0 copy-done.5
  337.1 8.1 %fusion.9 = f32[1536,192]{0,1:T(8,128)} fusion(bf16[3072,192]{0,1:T(8,128)(2,1)S(1)} %reduce_sum.75, f32[1536,192]{0,1:T(8,128)} %copy-done.6, f32[1536,192]{0,1:T(8,128)S(1)} %fusion.5, f32[1536]{0:T(1024)S(1)} %get-tuple-element.2, f32[192]{0:T(256)S(1)} %get-tuple-element.5, f32[1536]{0:T(1024)S(1)} %get-tuple-element.3, f32[1536]{0:T(1024)S(1)} %get-tuple-element.4, ...), kind=kOutput, calls=%fused_computation.20 | convolution fusion | flops 1830223872 | bytes 14194176 | tf_op jit(solution)/shard_map/dot_general | solution.py:69
  (8 shorter events, 0.1 us)
Async XLA Ops:
  7.2 95.7 %all-gather.7.cloned.1.call-start = ((), (), s32[]{:S(2)}) async-start(), calls=%async_computation | async-start | bytes 9732096 | tf_op jit(solution)/shard_map/all_gather | solution.py:37
  8.0 153.0 %all-gather.9.cloned.1.call-start = ((), (), s32[]{:S(2)}) async-start(), calls=%async_computation.1 | async-start | bytes 5898240 | tf_op jit(solution)/shard_map/all_gather | solution.py:41
  106.7 0.7 copy-start.1
  106.7 0.8 copy-start.4
  106.7 0.9 copy-start
  106.7 0.9 copy-start.3
  106.8 1.1 copy-start.2
  106.8 126.8 %all-gather.11.cloned.1.call-start = ((), (), s32[]{:S(2)}) async-start(), calls=%async_computation.2 | async-start | bytes 5898240 | tf_op jit(solution)/shard_map/all_gather | solution.py:9
  161.0 9.1 %slice-start = ((s8[9437184]{0:T(1024)(128)(4,1)}), s8[4194304]{0:T(1024)(128)(4,1)S(1)}, s32[]{:S(2)}) async-start(s8[9437184]{0:T(1024)(128)(4,1)} %bitcast.14), calls=%async_computation.4 | async-start | bytes 8388608
  163.6 6.5 %slice-start.1 = ((s8[9437184]{0:T(1024)(128)(4,1)}), s8[4194304]{0:T(1024)(128)(4,1)S(1)}, s32[]{:S(2)}) async-start(s8[9437184]{0:T(1024)(128)(4,1)} %bitcast.14), calls=%async_computation.5 | async-start | bytes 8388608
  163.6 6.5 %slice-start.2 = ((s8[9437184]{0:T(1024)(128)(4,1)}), s8[1048576]{0:T(1024)(128)(4,1)S(1)}, s32[]{:S(2)}) async-start(s8[9437184]{0:T(1024)(128)(4,1)} %bitcast.14), calls=%async_computation.6 | async-start | bytes 2097152
  170.1 167.0 %copy-start.5 = (f32[1536,192]{0,1:T(8,128)}, f32[1536,192]{0,1:T(8,128)S(1)}, u32[]{:S(2)}) copy-start(f32[1536,192]{0,1:T(8,128)S(1)} %fusion.5) | copy-start | bytes 3538948
  174.4 146.3 %all-gather.13.cloned.1.call-start = ((), (), s32[]{:S(2)}) async-start(), calls=%async_computation.3 | async-start | bytes 5898240 | tf_op jit(solution)/shard_map/all_gather | solution.py:9
  241.9 15.3 %slice-start.3 = ((s8[9437184]{0:T(1024)(128)(4,1)}), s8[1048576]{0:T(1024)(128)(4,1)S(1)}, s32[]{:S(2)}) async-start(s8[9437184]{0:T(1024)(128)(4,1)} %bitcast.16), calls=%async_computation.7 | async-start | bytes 2097152
  250.0 7.2 %slice-start.4 = ((s8[9437184]{0:T(1024)(128)(4,1)}), s8[4194304]{0:T(1024)(128)(4,1)S(1)}, s32[]{:S(2)}) async-start(s8[9437184]{0:T(1024)(128)(4,1)} %bitcast.16), calls=%async_computation.8 | async-start | bytes 8388608
  250.0 7.2 %slice-start.5 = ((s8[9437184]{0:T(1024)(128)(4,1)}), s8[4194304]{0:T(1024)(128)(4,1)S(1)}, s32[]{:S(2)}) async-start(s8[9437184]{0:T(1024)(128)(4,1)} %bitcast.16), calls=%async_computation.9 | async-start | bytes 8388608
  256.2 1.0 copy-start.6
Sparse Core Ops, SparseCore 0:
  9.9 92.9 all-gather.6
  106.9 53.9 all-gather.8
  174.6 59.0 all-gather.10
  261.7 59.0 all-gather.12
